TPU v7x, 32 devices: a whole 2x2x4 slice. The times are simulated.
32 devices in a mesh: gx: 2 (over y), gy: 8 (over z, core), gz: 2 (over x).
Axes of the slice: x: 2, y: 2, z: 4, core: 2. Of those that a mesh axis runs over, the one named last changes fastest.
Arguments:
- starting_kelvin: float32 [16, 32, 2048], P(None, 'gx', ('gy', 'gz')), may hold values from -6 to 6
- substance_label: int32 [16, 32, 2048], P(None, 'gx', ('gy', 'gz')), may hold values from 0 to 3
- voxel_source_patch: int32 [16, 32, 2048], P(None, 'gx', ('gy', 'gz')), may hold values from 0 to 15
- substance_traits: float32 [4, 4], replicated, may hold values from 0.5 to 2
- patch_source_intensity: float32 [16], replicated, may hold values from 0 to 8
Outputs:
- warmed_result: float32 [16, 32, 2048], P(None, 'gx', ('gy', 'gz'))
- solution: float32 [3, 16, 32, 2048], P(None, 'gz', 'gx', 'gy')
- residual: float32 [3, 16, 32, 2048], P(None, 'gz', 'gx', 'gy')
All inputs are finite; a program needn't handle non-finite values.
Results may differ from a plain program's by a relative error of at most 0.0029.
Values sent between devices are 32-bit elements; how exact they have to be, the bound alone decides.
A program may use at most 64 MiB of HBM per device.

v0:
```python
import jax
import jax.numpy as jnp
from jax import lax
from jax.sharding import PartitionSpec as P

ITERS = 3
time_step = 0.03
anchor_scale = 0.5
strain_gain = 2.0


def padded(value, sides, width):
    for axis, dim in sides:
        devices, length = (lax.axis_size(axis), value.shape[dim])
        up = [(i, (i + 1) % devices) for i in range(devices - 1)]
        down = [(j, i) for i, j in up]
        last = lax.slice_in_dim(value, length - width, length, axis=dim)
        initial = lax.slice_in_dim(value, 0, width, axis=dim)
        before = lax.ppermute(last, axis, up)
        after = lax.ppermute(initial, axis, down)
        value = jnp.concatenate([before, value, after], axis=dim)
    return value


def lookup(identity, table, count):
    summed = jnp.zeros(identity.shape, jnp.float32)
    for number in range(count):
        summed = summed + jnp.where(identity == number, table[number], jnp.float32(0.0))
    return summed


def conduct(own, other):
    return 2.0 * own * other / jnp.maximum(own + other, 0.25)


def heat_step(padded_temp, padded_cond, power, inverse_cap):
    centre = padded_temp[:, 1:-1, 1:-1]
    own = padded_cond[:, 1:-1, 1:-1]
    layers, rows, columns = centre.shape
    heat_flux = jnp.zeros_like(centre)
    for row_offset, column_offset in ((0, 1), (2, 1), (1, 0), (1, 2)):
        neighbour = padded_temp[
            :, row_offset : row_offset + rows, column_offset : column_offset + columns
        ]
        other = padded_cond[
            :, row_offset : row_offset + rows, column_offset : column_offset + columns
        ]
        heat_flux = heat_flux + conduct(own, other) * (neighbour - centre)
    vertical_temp = jnp.pad(centre, ((1, 1), (0, 0), (0, 0)))
    vertical_cond = jnp.pad(own, ((1, 1), (0, 0), (0, 0)))
    for layer_offset in (0, 2):
        other = vertical_cond[layer_offset : layer_offset + layers]
        neighbour = vertical_temp[layer_offset : layer_offset + layers]
        heat_flux = heat_flux + conduct(own, other) * (neighbour - centre)
    return centre + time_step * inverse_cap * (heat_flux + power)


def neighbour_offsets():
    listed = []
    for along_z in (-1, 0, 1):
        for along_x in (-1, 0, 1):
            for along_y in (-1, 0, 1):
                if along_z != 0 or along_x != 0 or along_y != 0:
                    listed.append((along_z, along_x, along_y))
    return listed


def apply_operator(field, padded_field, modulus, padded_modulus):
    layers, rows, columns = modulus.shape
    parts = [
        anchor_scale * modulus * field[0],
        anchor_scale * modulus * field[1],
        anchor_scale * modulus * field[2],
    ]
    for along_z, along_x, along_y in neighbour_offsets():
        length_sq = along_z * along_z + along_x * along_x + along_y * along_y
        window = (
            slice(1 + along_z, 1 + along_z + layers),
            slice(1 + along_x, 1 + along_x + rows),
            slice(1 + along_y, 1 + along_y + columns),
        )
        weight = 0.5 / length_sq * (modulus + padded_modulus[window])
        change = [field[index_c] - padded_field[index_c][window] for index_c in range(3)]
        projected = (along_z * change[0] + along_x * change[1] + along_y * change[2]) / length_sq
        for index_c, direction_part in enumerate((along_z, along_x, along_y)):
            parts[index_c] = parts[index_c] + weight * (
                0.5 * change[index_c] + direction_part * projected
            )
    return jnp.stack(parts)


def thermal_load(modulus, padded_modulus, strain, padded_strain):
    layers, rows, columns = modulus.shape
    parts = [jnp.zeros_like(modulus), jnp.zeros_like(modulus), jnp.zeros_like(modulus)]
    for along_z, along_x, along_y in neighbour_offsets():
        length_sq = along_z * along_z + along_x * along_x + along_y * along_y
        window = (
            slice(1 + along_z, 1 + along_z + layers),
            slice(1 + along_x, 1 + along_x + rows),
            slice(1 + along_y, 1 + along_y + columns),
        )
        weight = 0.5 / length_sq * (modulus + padded_modulus[window])
        pushing = weight * (0.5 * (strain + padded_strain[window]))
        for index_c, direction_part in enumerate((along_z, along_x, along_y)):
            if direction_part != 0:
                parts[index_c] = parts[index_c] - strain_gain * direction_part * pushing
    return jnp.stack(parts)


def two_products(residual, image):
    return lax.psum((jnp.sum(residual * residual), jnp.sum(residual * image)), ("gx", "gy", "gz"))


def per_device(
    starting_kelvin, substance_label, voxel_source_patch, substance_traits, patch_source_intensity
):
    count = substance_traits.shape[1]
    diffusive_coefficient = lookup(substance_label, substance_traits[0], count)
    inverse_cap = 1.0 / lookup(substance_label, substance_traits[1], count)
    power = lookup(voxel_source_patch, patch_source_intensity, patch_source_intensity.shape[0])
    padded_array = padded(
        jnp.stack([starting_kelvin, diffusive_coefficient]), (("gx", 2), (("gy", "gz"), 3)), 1
    )
    padded_cond = padded_array[1]
    warmed_result = heat_step(padded_array[0], padded_cond, power, inverse_cap)
    number = 0
    extended = padded(warmed_result, (("gx", 1), (("gy", "gz"), 2)), 1)
    warmed_result = heat_step(extended, padded_cond, power, inverse_cap)
    modulus = lookup(substance_label, substance_traits[2], count)
    strain = lookup(substance_label, substance_traits[3], count) * warmed_result
    fields = jnp.stack([modulus, strain])
    vertical_cycle = ((0, 0), (1, 1), (0, 0), (0, 0))
    padded_fields = jnp.pad(padded(fields, (("gx", 2), (("gy", "gz"), 3)), 1), vertical_cycle)

    def extend(field):
        return jnp.pad(padded(field, (("gx", 2), (("gy", "gz"), 3)), 1), vertical_cycle)

    modulus = fields[0]
    padded_modulus = padded_fields[0]
    load = thermal_load(modulus, padded_modulus, fields[1], padded_fields[1])

    def operate(field):
        return apply_operator(field, extend(field), modulus, padded_modulus)

    solution = jnp.zeros_like(load)
    residual = load
    image = operate(residual)
    norm_now, product = two_products(residual, image)
    alpha = norm_now / product
    direction, along_image = (residual, image)
    for number in range(ITERS):
        solution = solution + alpha * direction
        residual = residual - alpha * along_image
        if number + 1 < ITERS:
            image = operate(residual)
            norm_next, product = two_products(residual, image)
            ratio = norm_next / norm_now
            alpha = norm_next / (product - ratio * norm_next / alpha)
            direction = residual + ratio * direction
            along_image = image + ratio * along_image
            norm_now = norm_next
    joined = lax.all_to_all(
        jnp.concatenate([solution, residual]), "gz", split_axis=1, concat_axis=3, tiled=True
    )
    solution = joined[:3]
    residual = joined[3:]
    return (warmed_result, solution, residual)


def solution(mesh):
    in_specs = (
        P(None, "gx", ("gy", "gz")),
        P(None, "gx", ("gy", "gz")),
        P(None, "gx", ("gy", "gz")),
        P(),
        P(),
    )
    out_specs = (P(None, "gx", ("gy", "gz")), P(None, "gz", "gx", "gy"), P(None, "gz", "gx", "gy"))
    return jax.shard_map(
        per_device, mesh=mesh, in_specs=in_specs, out_specs=out_specs, check_vma=False
    )
```

profile of v0, /device:TPU:0, one launch (start us, length us, event | category | flops | bytes accessed | tf_op | source)
XLA Modules:
  0.0 370.7 jit_solution(7479689364601131842)
XLA Ops:
  0.6 2.0 fusion.181
  2.6 3.5 fusion.168
  6.1 3.5 copy_bitcast_fusion
  9.6 4.9 %collective-permute-start = (f32[2,16,1,128]{3,1,2,0:T(8,128)S(1)}, f32[2,16,1,128]{3,1,2,0:T(8,128)S(1)}, u32[]{:S(2)}, u32[]{:S(2)}) collective-permute-start(f32[2,16,1,128]{3,1,2,0:T(8,128)S(1)} %get-tuple-element.112), channel_id=1, source_target_pairs={{0,16},{1,17},{2,18},{3,19},{4,20},{5,21},{6,22},{7,23},{8,24},{9,... | collective-permute-start | bytes 49160 | tf_op jit(solution)/shard_map/ppermute | solution.py:19
  15.9 4.2 %collective-permute-done.1 = f32[2,16,1,128]{3,1,2,0:T(8,128)S(1)} collective-permute-done((f32[2,16,1,128]{3,1,2,0:T(8,128)S(1)}, f32[2,16,1,128]{3,1,2,0:T(8,128)S(1)}, u32[]{:S(2)}, u32[]{:S(2)}) %collective-permute-start.1) | collective-permute-done | bytes 16416 | tf_op jit(solution)/shard_map/ppermute | solution.py:20
  20.3 3.4 collective-permute-start.2
  25.8 8.3 %collective-permute-done.2 = f32[2,16,18,1]{3,1,2,0:T(8,128)S(1)} collective-permute-done((f32[2,16,18,1]{3,1,2,0:T(8,128)S(1)}, f32[2,16,18,1]{3,1,2,0:T(8,128)S(1)}, u32[]{:S(2)}, u32[]{:S(2)}) %collective-permute-start.2) | collective-permute-done | bytes 2336 | tf_op jit(solution)/shard_map/ppermute | solution.py:19
  35.3 13.0 %fusion.8 = f32[16,16,128]{2,0,1:T(8,128)S(1)} fusion(f32[16,16,128]{2,0,1:T(8,128)S(1)} %slice.2049, f32[16,18,130]{2,0,1:T(8,128)S(1)} %get-tuple-element.91, pred[16,16,128]{2,0,1:T(8,128)(4,1)S(1)} %get-tuple-element.74, f32[]{:T(128)} %bitcast.10, pred[16,16,128]{2,0,1:T(8,128)(4,1)S(1)} %get-tuple-element.73, f32[]{:T(128)} %bitcast.9, ...), kind=kLoop, calls=%fused_computation.73 | loop fusion | flops 3342336 | bytes 1835088 | tf_op jit(solution)/shard_map/add | solution.py:55
  48.3 1.6 collective-permute-start.4
  51.3 4.2 %collective-permute-done.5 = f32[16,1,128]{2,0,1:T(8,128)S(1)} collective-permute-done((f32[16,1,128]{2,0,1:T(8,128)S(1)}, f32[16,1,128]{2,0,1:T(8,128)S(1)}, u32[]{:S(2)}, u32[]{:S(2)}) %collective-permute-start.5) | collective-permute-done | bytes 8224 | tf_op jit(solution)/shard_map/ppermute | solution.py:20
  55.6 4.8 %collective-permute-start.6 = (f32[16,18,1]{2,0,1:T(8,128)S(1)}, f32[16,18,1]{2,0,1:T(8,128)S(1)}, u32[]{:S(2)}, u32[]{:S(2)}) collective-permute-start(f32[16,18,1]{2,0,1:T(8,128)S(1)} %get-tuple-element.114), channel_id=1, source_target_pairs={{0,1},{1,2},{2,3},{3,4},{4,5},{5,6},{6,7},{7,8},{8,9},{9,10},{10,1... | collective-permute-start | bytes 3464 | tf_op jit(solution)/shard_map/ppermute | solution.py:19
  61.7 1.6 collective-permute-done.6
  63.3 5.1 %collective-permute-done.7 = f32[16,18,1]{2,0,1:T(8,128)S(1)} collective-permute-done((f32[16,18,1]{2,0,1:T(8,128)S(1)}, f32[16,18,1]{2,0,1:T(8,128)S(1)}, u32[]{:S(2)}, u32[]{:S(2)}) %collective-permute-start.7) | collective-permute-done | bytes 1184 | tf_op jit(solution)/shard_map/ppermute | solution.py:20
  68.3 15.6 %add_multiply_fusion.6 = (f32[16,16,128]{2,0,1:T(8,128)S(1)}, f32[16,16,128]{2,0,1:T(8,128)S(1)}) fusion(pred[16,16,128]{2,0,1:T(8,128)(4,1)S(1)} %get-tuple-element.74, pred[16,16,128]{2,0,1:T(8,128)(4,1)S(1)} %get-tuple-element.73, pred[16,16,128]{2,0,1:T(8,128)(4,1)S(1)} %get-tuple-element.72, pred[16,16,128]{2,0,1:T(8,128)(4,1)S(1)} %get-tuple-element.71, ...), kind=kLoop, calls=%fused_computation.625 | loop fusion | flops 3866624 | bytes 1460576 | tf_op jit(solution)/shard_map/mul | solution.py:130
  83.9 1.6 collective-permute-start.8
  87.0 4.2 %collective-permute-done.9 = f32[2,16,1,128]{3,1,2,0:T(8,128)S(1)} collective-permute-done((f32[2,16,1,128]{3,1,2,0:T(8,128)S(1)}, f32[2,16,1,128]{3,1,2,0:T(8,128)S(1)}, u32[]{:S(2)}, u32[]{:S(2)}) %collective-permute-start.9) | collective-permute-done | bytes 16416 | tf_op jit(solution)/shard_map/ppermute | solution.py:20
  94.1 5.2 %collective-permute-done.10 = f32[2,16,18,1]{3,1,2,0:T(8,128)S(1)} collective-permute-done((f32[2,16,18,1]{3,1,2,0:T(8,128)S(1)}, f32[2,16,18,1]{3,1,2,0:T(8,128)S(1)}, u32[]{:S(2)}, u32[]{:S(2)}) %collective-permute-start.10) | collective-permute-done | bytes 2336 | tf_op jit(solution)/shard_map/ppermute | solution.py:19
  99.3 4.7 %collective-permute-done.11 = f32[2,16,18,1]{3,1,2,0:T(8,128)S(1)} collective-permute-done((f32[2,16,18,1]{3,1,2,0:T(8,128)S(1)}, f32[2,16,18,1]{3,1,2,0:T(8,128)S(1)}, u32[]{:S(2)}, u32[]{:S(2)}) %collective-permute-start.11) | collective-permute-done | bytes 2336 | tf_op jit(solution)/shard_map/ppermute | solution.py:20
  104.4 3.4 fusion.31
  107.8 3.4 fusion.52
  111.3 3.4 fusion.93
  114.7 2.2 collective-permute-start.12
  118.4 4.2 %collective-permute-done.13 = f32[3,16,1,128]{3,1,2,0:T(8,128)S(1)} collective-permute-done((f32[3,16,1,128]{3,1,2,0:T(8,128)S(1)}, f32[3,16,1,128]{3,1,2,0:T(8,128)S(1)}, u32[]{:S(2)}, u32[]{:S(2)}) %collective-permute-start.13) | collective-permute-done | bytes 24608 | tf_op jit(solution)/shard_map/ppermute | solution.py:20
  123.3 6.3 %collective-permute-start.14 = (f32[3,16,18,1]{2,1,3,0:T(8,128)S(1)}, f32[3,16,18,1]{2,1,3,0:T(8,128)S(1)}, u32[]{:S(2)}, u32[]{:S(2)}) collective-permute-start(f32[3,16,18,1]{2,1,3,0:T(8,128)S(1)} %copy.174), channel_id=1, source_target_pairs={{0,1},{1,2},{2,3},{3,4},{4,5},{5,6},{6,7},{7,8},{8,9},{9,10},{10,1... | collective-permute-start | bytes 10376 | tf_op jit(solution)/shard_map/ppermute | solution.py:19
  131.9 3.9 %collective-permute-done.15 = f32[3,16,18,1]{2,1,3,0:T(8,128)S(1)} collective-permute-done((f32[3,16,18,1]{2,1,3,0:T(8,128)S(1)}, f32[3,16,18,1]{2,1,3,0:T(8,128)S(1)}, u32[]{:S(2)}, u32[]{:S(2)}) %collective-permute-start.15) | collective-permute-done | bytes 3488 | tf_op jit(solution)/shard_map/ppermute | solution.py:20
  137.0 5.2 %add_bitcast_fusion.7 = f32[1,16,16,128]{3,1,2,0:T(8,128)S(1)} fusion(f32[16,16,128]{2,0,1:T(8,128)S(1)} %fusion.52, f32[16,16,128]{2,0,1:T(8,128)S(1)} %fusion.93, f32[18,18,130]{2,0,1:T(8,128)S(1)} %get-tuple-element.85, f32[18,18,130]{2,0,1:T(8,128)S(1)} %get-tuple-element.84, f32[16,16,128]{2,0,1:T(8,128)S(1)} %fusion.31, ...), kind=kLoop, calls=%fused_computation.599 | loop fusion | flops 11862016 | bytes 14286864 | tf_op jit(solution)/shard_map/stack | solution.py:89
  142.2 5.2 %add_bitcast_fusion.6 = f32[1,16,16,128]{3,1,2,0:T(8,128)S(1)} fusion(f32[16,16,128]{2,0,1:T(8,128)S(1)} %fusion.31, f32[16,16,128]{2,0,1:T(8,128)S(1)} %fusion.93, f32[18,18,130]{2,0,1:T(8,128)S(1)} %get-tuple-element.85, f32[16,16,128]{2,0,1:T(8,128)S(1)} %fusion.52, f32[18,18,130]{2,0,1:T(8,128)S(1)} %get-tuple-element.84, ...), kind=kLoop, calls=%fused_computation.598 | loop fusion | flops 11862016 | bytes 14286864 | tf_op jit(solution)/shard_map/stack | solution.py:89
  147.4 5.2 %add_bitcast_fusion.8 = f32[1,16,16,128]{3,1,2,0:T(8,128)S(1)} fusion(f32[16,16,128]{2,0,1:T(8,128)S(1)} %fusion.93, f32[18,18,130]{2,0,1:T(8,128)S(1)} %get-tuple-element.85, f32[16,16,128]{2,0,1:T(8,128)S(1)} %fusion.52, f32[18,18,130]{2,0,1:T(8,128)S(1)} %get-tuple-element.84, f32[16,16,128]{2,0,1:T(8,128)S(1)} %fusion.31, ...), kind=kLoop, calls=%fused_computation.600 | loop fusion | flops 11862016 | bytes 14286864 | tf_op jit(solution)/shard_map/stack | solution.py:89
  153.3 40.6 %all-reduce.9 = (f32[]{:T(128)}, f32[]{:T(128)}) all-reduce(f32[]{:T(128)} %get-tuple-element.17, f32[]{:T(128)} %get-tuple-element.16), channel_id=1, replica_groups=mesh['gx'=2,'gy'=8,'gz'=2] {'gx','gy','gz'}, use_global_device_ids=true, to_apply=%region_1.2 | all-reduce | flops 2 | bytes 16 | tf_op jit(solution)/shard_map/psum | solution.py:111
  195.3 4.4 %collective-permute-start.16 = (f32[3,16,1,128]{3,1,2,0:T(8,128)S(1)}, f32[3,16,1,128]{3,1,2,0:T(8,128)S(1)}, u32[]{:S(2)}, u32[]{:S(2)}) collective-permute-start(f32[3,16,1,128]{3,1,2,0:T(8,128)S(1)} %get-tuple-element.102), channel_id=1, source_target_pairs={{0,16},{1,17},{2,18},{3,19},{4,20},{5,21},{6,22},{7,23},{8,24},{9,... | collective-permute-start | bytes 73736 | tf_op jit(solution)/shard_map/ppermute | solution.py:19
  201.2 4.2 %collective-permute-done.17 = f32[3,16,1,128]{3,1,2,0:T(8,128)S(1)} collective-permute-done((f32[3,16,1,128]{3,1,2,0:T(8,128)S(1)}, f32[3,16,1,128]{3,1,2,0:T(8,128)S(1)}, u32[]{:S(2)}, u32[]{:S(2)}) %collective-permute-start.17) | collective-permute-done | bytes 24608 | tf_op jit(solution)/shard_map/ppermute | solution.py:20
  206.0 2.0 collective-permute-start.18
  210.4 3.8 %collective-permute-done.19 = f32[3,16,18,1]{2,1,3,0:T(8,128)S(1)} collective-permute-done((f32[3,16,18,1]{2,1,3,0:T(8,128)S(1)}, f32[3,16,18,1]{2,1,3,0:T(8,128)S(1)}, u32[]{:S(2)}, u32[]{:S(2)}) %collective-permute-start.19) | collective-permute-done | bytes 3488 | tf_op jit(solution)/shard_map/ppermute | solution.py:20
  215.3 5.4 %add_bitcast_fusion.5 = (f32[1,16,16,128]{3,1,2,0:T(8,128)S(1)}, f32[16,16,128]{2,0,1:T(8,128)S(1)}, f32[16,16,128]{2,0,1:T(8,128)S(1)}, f32[16,16,128]{2,0,1:T(...) fusion(f32[18,18,130]{2,0,1:T(8,128)S(1)} %get-tuple-element.82, ...), kind=kLoop, calls=%fused_computation.573 | loop fusion | flops 11862016 | bytes 17170448 | tf_op jit(solution)/shard_map/stack | solution.py:89
  220.7 4.1 %add_bitcast_fusion.4 = f32[1,16,16,128]{3,1,2,0:T(8,128)S(1)} fusion(f32[16,16,128]{2,0,1:T(8,128)S(1)} %get-tuple-element.69, f32[16,16,128]{2,0,1:T(8,128)S(1)} %get-tuple-element.51, f32[16,16,128]{2,0,1:T(8,128)S(1)} %get-tuple-element.66, f32[16,16,128]{2,0,1:T(8,128)S(1)} %get-tuple-element.50, f32[16,16,128]{2,0,1:T(8,128)S(1)} %get-tuple-element.65, ...), kind=kLoop, calls=%fused_computation.572 | loop fusion | flops 7864320 | bytes 11403280 | tf_op jit(solution)/shard_map/stack | solution.py:89
  224.8 4.1 %add_bitcast_fusion.3 = f32[1,16,16,128]{3,1,2,0:T(8,128)S(1)} fusion(f32[16,16,128]{2,0,1:T(8,128)S(1)} %get-tuple-element.69, f32[16,16,128]{2,0,1:T(8,128)S(1)} %get-tuple-element.68, f32[16,16,128]{2,0,1:T(8,128)S(1)} %get-tuple-element.67, f32[16,16,128]{2,0,1:T(8,128)S(1)} %get-tuple-element.66, f32[16,16,128]{2,0,1:T(8,128)S(1)} %get-tuple-element.65, ...), kind=kLoop, calls=%fused_computation.571 | loop fusion | flops 7864320 | bytes 11403280 | tf_op jit(solution)/shard_map/stack | solution.py:89
  229.7 39.7 %all-reduce.8 = (f32[]{:T(128)}, f32[]{:T(128)}) all-reduce(f32[]{:T(128)} %get-tuple-element.15, f32[]{:T(128)} %get-tuple-element.14), channel_id=1, replica_groups=mesh['gx'=2,'gy'=8,'gz'=2] {'gx','gy','gz'}, use_global_device_ids=true, to_apply=%region_5.6 | all-reduce | flops 2 | bytes 16 | tf_op jit(solution)/shard_map/psum | solution.py:111
  274.2 4.4 %collective-permute-start.20 = (f32[3,16,1,128]{3,1,2,0:T(8,128)S(1)}, f32[3,16,1,128]{3,1,2,0:T(8,128)S(1)}, u32[]{:S(2)}, u32[]{:S(2)}) collective-permute-start(f32[3,16,1,128]{3,1,2,0:T(8,128)S(1)} %get-tuple-element.100), channel_id=1, source_target_pairs={{0,16},{1,17},{2,18},{3,19},{4,20},{5,21},{6,22},{7,23},{8,24},{9,... | collective-permute-start | bytes 73736 | tf_op jit(solution)/shard_map/ppermute | solution.py:19
  280.1 4.2 %collective-permute-done.21 = f32[3,16,1,128]{3,1,2,0:T(8,128)S(1)} collective-permute-done((f32[3,16,1,128]{3,1,2,0:T(8,128)S(1)}, f32[3,16,1,128]{3,1,2,0:T(8,128)S(1)}, u32[]{:S(2)}, u32[]{:S(2)}) %collective-permute-start.21) | collective-permute-done | bytes 24608 | tf_op jit(solution)/shard_map/ppermute | solution.py:20
  285.0 1.9 collective-permute-start.22
  287.3 1.5 collective-permute-start.23
  289.3 3.7 %collective-permute-done.23 = f32[3,16,18,1]{2,1,3,0:T(8,128)S(1)} collective-permute-done((f32[3,16,18,1]{2,1,3,0:T(8,128)S(1)}, f32[3,16,18,1]{2,1,3,0:T(8,128)S(1)}, u32[]{:S(2)}, u32[]{:S(2)}) %collective-permute-start.23) | collective-permute-done | bytes 3488 | tf_op jit(solution)/shard_map/ppermute | solution.py:20
  294.1 5.4 %add_bitcast_fusion.2 = (f32[1,16,16,128]{3,1,2,0:T(8,128)S(1)}, f32[16,16,128]{2,0,1:T(8,128)S(1)}, f32[16,16,128]{2,0,1:T(8,128)S(1)}, f32[16,16,128]{2,0,1:T(...) fusion(f32[18,18,130]{2,0,1:T(8,128)S(1)} %get-tuple-element.79, ...), kind=kLoop, calls=%fused_computation.546 | loop fusion | flops 11862016 | bytes 17170448 | tf_op jit(solution)/shard_map/stack | solution.py:89
  299.5 4.1 %add_bitcast_fusion.1 = f32[1,16,16,128]{3,1,2,0:T(8,128)S(1)} fusion(f32[16,16,128]{2,0,1:T(8,128)S(1)} %get-tuple-element.46, f32[16,16,128]{2,0,1:T(8,128)S(1)} %get-tuple-element.28, f32[16,16,128]{2,0,1:T(8,128)S(1)} %get-tuple-element.43, f32[16,16,128]{2,0,1:T(8,128)S(1)} %get-tuple-element.27, f32[16,16,128]{2,0,1:T(8,128)S(1)} %get-tuple-element.42, ...), kind=kLoop, calls=%fused_computation.545 | loop fusion | flops 7864320 | bytes 11403280 | tf_op jit(solution)/shard_map/stack | solution.py:89
  303.6 4.1 %add_bitcast_fusion = f32[1,16,16,128]{3,1,2,0:T(8,128)S(1)} fusion(f32[16,16,128]{2,0,1:T(8,128)S(1)} %get-tuple-element.46, f32[16,16,128]{2,0,1:T(8,128)S(1)} %get-tuple-element.45, f32[16,16,128]{2,0,1:T(8,128)S(1)} %get-tuple-element.44, f32[16,16,128]{2,0,1:T(8,128)S(1)} %get-tuple-element.43, f32[16,16,128]{2,0,1:T(8,128)S(1)} %get-tuple-element.42, ...), kind=kLoop, calls=%fused_computation.544 | loop fusion | flops 7864320 | bytes 11403280 | tf_op jit(solution)/shard_map/stack | solution.py:89
  308.6 39.8 %all-reduce.7 = (f32[]{:T(128)}, f32[]{:T(128)}) all-reduce(f32[]{:T(128)} %get-tuple-element.13, f32[]{:T(128)} %get-tuple-element.12), channel_id=1, replica_groups=mesh['gx'=2,'gy'=8,'gz'=2] {'gx','gy','gz'}, use_global_device_ids=true, to_apply=%region_9.10 | all-reduce | flops 2 | bytes 16 | tf_op jit(solution)/shard_map/psum | solution.py:111
  353.9 3.5 all-to-all-start
  358.2 9.7 %all-to-all-done = f32[6,16,16,128]{3,2,0,1:T(8,128)S(1)} async-done(((f32[6,16,16,128]{3,2,0,1:T(8,128)}), f32[6,16,16,128]{3,2,0,1:T(8,128)S(1)}, u32[]{:S(2)}, u32[]{:S(2)}) %all-to-all-start) | async-done | bytes 786464 | tf_op jit(solution)/shard_map/all_to_all | solution.py:162
  (84 shorter events, 34.8 us)
Async XLA Ops:
  6.1 19.0 %copy-start.1 = (f32[16]{0:T(128)S(1)}, f32[16]{0:T(128)}, u32[]{:S(2)}) copy-start(f32[16]{0:T(128)} %param.9) | copy-start | bytes 196
  9.6 6.3 %collective-permute-start = (f32[2,16,1,128]{3,1,2,0:T(8,128)S(1)}, f32[2,16,1,128]{3,1,2,0:T(8,128)S(1)}, u32[]{:S(2)}, u32[]{:S(2)}) collective-permute-start(f32[2,16,1,128]{3,1,2,0:T(8,128)S(1)} %get-tuple-element.112), channel_id=1, source_target_pairs={{0,16},{1,17},{2,18},{3,19},{4,20},{5,21},{6,22},{7,23},{8,24},{9,... | collective-permute-start | bytes 49160 | tf_op jit(solution)/shard_map/ppermute | solution.py:19
  14.5 5.6 %collective-permute-start.1 = (f32[2,16,1,128]{3,1,2,0:T(8,128)S(1)}, f32[2,16,1,128]{3,1,2,0:T(8,128)S(1)}, u32[]{:S(2)}, u32[]{:S(2)}) collective-permute-start(f32[2,16,1,128]{3,1,2,0:T(8,128)S(1)} %get-tuple-element.113), channel_id=1, source_target_pairs={{16,0},{17,1},{18,2},{19,3},{20,4},{21,5},{22,6},{23,7},{24,8},{25... | collective-permute-start | bytes 49160 | tf_op jit(solution)/shard_map/ppermute | solution.py:20
  20.3 13.8 %collective-permute-start.2 = (f32[2,16,18,1]{3,1,2,0:T(8,128)S(1)}, f32[2,16,18,1]{3,1,2,0:T(8,128)S(1)}, u32[]{:S(2)}, u32[]{:S(2)}) collective-permute-start(f32[2,16,18,1]{3,1,2,0:T(8,128)S(1)} %get-tuple-element.108), channel_id=1, source_target_pairs={{0,1},{1,2},{2,3},{3,4},{4,5},{5,6},{6,7},{7,8},{8,9},{9,10},{10,1... | collective-permute-start | bytes 6920 | tf_op jit(solution)/shard_map/ppermute | solution.py:19
  23.7 11.0 %collective-permute-start.3 = (f32[2,16,18,1]{3,1,2,0:T(8,128)S(1)}, f32[2,16,18,1]{3,1,2,0:T(8,128)S(1)}, u32[]{:S(2)}, u32[]{:S(2)}) collective-permute-start(f32[2,16,18,1]{3,1,2,0:T(8,128)S(1)} %get-tuple-element.109), channel_id=1, source_target_pairs={{1,0},{2,1},{3,2},{4,3},{5,4},{6,5},{7,6},{8,7},{9,8},{10,9},{11,1... | collective-permute-start | bytes 6920 | tf_op jit(solution)/shard_map/ppermute | solution.py:20
  25.8 9.5 %copy-start = (s32[16,16,128]{2,1,0:T(8,128)S(1)}, s32[16,16,128]{2,1,0:T(8,128)}, u32[]{:S(2)}) copy-start(s32[16,16,128]{2,1,0:T(8,128)} %param.7) | copy-start | bytes 393220
  48.3 3.0 collective-permute-start.4
  49.9 5.5 %collective-permute-start.5 = (f32[16,1,128]{2,0,1:T(8,128)S(1)}, f32[16,1,128]{2,0,1:T(8,128)S(1)}, u32[]{:S(2)}, u32[]{:S(2)}) collective-permute-start(f32[16,1,128]{2,0,1:T(8,128)S(1)} %get-tuple-element.117), channel_id=1, source_target_pairs={{16,0},{17,1},{18,2},{19,3},{20,4},{21,5},{22,6},{23,7},{24,8},{25... | collective-permute-start | bytes 24584 | tf_op jit(solution)/shard_map/ppermute | solution.py:20
  55.6 7.7 %collective-permute-start.6 = (f32[16,18,1]{2,0,1:T(8,128)S(1)}, f32[16,18,1]{2,0,1:T(8,128)S(1)}, u32[]{:S(2)}, u32[]{:S(2)}) collective-permute-start(f32[16,18,1]{2,0,1:T(8,128)S(1)} %get-tuple-element.114), channel_id=1, source_target_pairs={{0,1},{1,2},{2,3},{3,4},{4,5},{5,6},{6,7},{7,8},{8,9},{9,10},{10,1... | collective-permute-start | bytes 3464 | tf_op jit(solution)/shard_map/ppermute | solution.py:19
  60.4 7.9 %collective-permute-start.7 = (f32[16,18,1]{2,0,1:T(8,128)S(1)}, f32[16,18,1]{2,0,1:T(8,128)S(1)}, u32[]{:S(2)}, u32[]{:S(2)}) collective-permute-start(f32[16,18,1]{2,0,1:T(8,128)S(1)} %get-tuple-element.115), channel_id=1, source_target_pairs={{1,0},{2,1},{3,2},{4,3},{5,4},{6,5},{7,6},{8,7},{9,8},{10,9},{11,1... | collective-permute-start | bytes 3464 | tf_op jit(solution)/shard_map/ppermute | solution.py:20
  83.9 3.1 collective-permute-start.8
  85.5 5.6 %collective-permute-start.9 = (f32[2,16,1,128]{3,1,2,0:T(8,128)S(1)}, f32[2,16,1,128]{3,1,2,0:T(8,128)S(1)}, u32[]{:S(2)}, u32[]{:S(2)}) collective-permute-start(f32[2,16,1,128]{3,1,2,0:T(8,128)S(1)} %get-tuple-element.111), channel_id=1, source_target_pairs={{16,0},{17,1},{18,2},{19,3},{20,4},{21,5},{22,6},{23,7},{24,8},{25... | collective-permute-start | bytes 49160 | tf_op jit(solution)/shard_map/ppermute | solution.py:20
  91.4 7.9 %collective-permute-start.10 = (f32[2,16,18,1]{3,1,2,0:T(8,128)S(1)}, f32[2,16,18,1]{3,1,2,0:T(8,128)S(1)}, u32[]{:S(2)}, u32[]{:S(2)}) collective-permute-start(f32[2,16,18,1]{3,1,2,0:T(8,128)S(1)} %get-tuple-element.106), channel_id=1, source_target_pairs={{0,1},{1,2},{2,3},{3,4},{4,5},{5,6},{6,7},{7,8},{8,9},{9,10},{10,1... | collective-permute-start | bytes 6920 | tf_op jit(solution)/shard_map/ppermute | solution.py:19
  92.8 11.1 %collective-permute-start.11 = (f32[2,16,18,1]{3,1,2,0:T(8,128)S(1)}, f32[2,16,18,1]{3,1,2,0:T(8,128)S(1)}, u32[]{:S(2)}, u32[]{:S(2)}) collective-permute-start(f32[2,16,18,1]{3,1,2,0:T(8,128)S(1)} %get-tuple-element.107), channel_id=1, source_target_pairs={{1,0},{2,1},{3,2},{4,3},{5,4},{6,5},{7,6},{8,7},{9,8},{10,9},{11,1... | collective-permute-start | bytes 6920 | tf_op jit(solution)/shard_map/ppermute | solution.py:20
  114.7 3.7 %collective-permute-start.12 = (f32[3,16,1,128]{3,1,2,0:T(8,128)S(1)}, f32[3,16,1,128]{3,1,2,0:T(8,128)S(1)}, u32[]{:S(2)}, u32[]{:S(2)}) collective-permute-start(f32[3,16,1,128]{3,1,2,0:T(8,128)S(1)} %get-tuple-element.104), channel_id=1, source_target_pairs={{0,16},{1,17},{2,18},{3,19},{4,20},{5,21},{6,22},{7,23},{8,24},{9,... | collective-permute-start | bytes 73736 | tf_op jit(solution)/shard_map/ppermute | solution.py:19
  116.9 5.7 %collective-permute-start.13 = (f32[3,16,1,128]{3,1,2,0:T(8,128)S(1)}, f32[3,16,1,128]{3,1,2,0:T(8,128)S(1)}, u32[]{:S(2)}, u32[]{:S(2)}) collective-permute-start(f32[3,16,1,128]{3,1,2,0:T(8,128)S(1)} %get-tuple-element.105), channel_id=1, source_target_pairs={{16,0},{17,1},{18,2},{19,3},{20,4},{21,5},{22,6},{23,7},{24,8},{25... | collective-permute-start | bytes 73736 | tf_op jit(solution)/shard_map/ppermute | solution.py:20
  123.3 8.2 %collective-permute-start.14 = (f32[3,16,18,1]{2,1,3,0:T(8,128)S(1)}, f32[3,16,18,1]{2,1,3,0:T(8,128)S(1)}, u32[]{:S(2)}, u32[]{:S(2)}) collective-permute-start(f32[3,16,18,1]{2,1,3,0:T(8,128)S(1)} %copy.174), channel_id=1, source_target_pairs={{0,1},{1,2},{2,3},{3,4},{4,5},{5,6},{6,7},{7,8},{8,9},{9,10},{10,1... | collective-permute-start | bytes 10376 | tf_op jit(solution)/shard_map/ppermute | solution.py:19
  130.0 5.8 %collective-permute-start.15 = (f32[3,16,18,1]{2,1,3,0:T(8,128)S(1)}, f32[3,16,18,1]{2,1,3,0:T(8,128)S(1)}, u32[]{:S(2)}, u32[]{:S(2)}) collective-permute-start(f32[3,16,18,1]{2,1,3,0:T(8,128)S(1)} %copy.175), channel_id=1, source_target_pairs={{1,0},{2,1},{3,2},{4,3},{5,4},{6,5},{7,6},{8,7},{9,8},{10,9},{11,1... | collective-permute-start | bytes 10376 | tf_op jit(solution)/shard_map/ppermute | solution.py:20
  195.3 5.9 %collective-permute-start.16 = (f32[3,16,1,128]{3,1,2,0:T(8,128)S(1)}, f32[3,16,1,128]{3,1,2,0:T(8,128)S(1)}, u32[]{:S(2)}, u32[]{:S(2)}) collective-permute-start(f32[3,16,1,128]{3,1,2,0:T(8,128)S(1)} %get-tuple-element.102), channel_id=1, source_target_pairs={{0,16},{1,17},{2,18},{3,19},{4,20},{5,21},{6,22},{7,23},{8,24},{9,... | collective-permute-start | bytes 73736 | tf_op jit(solution)/shard_map/ppermute | solution.py:19
  199.7 5.7 %collective-permute-start.17 = (f32[3,16,1,128]{3,1,2,0:T(8,128)S(1)}, f32[3,16,1,128]{3,1,2,0:T(8,128)S(1)}, u32[]{:S(2)}, u32[]{:S(2)}) collective-permute-start(f32[3,16,1,128]{3,1,2,0:T(8,128)S(1)} %get-tuple-element.103), channel_id=1, source_target_pairs={{16,0},{17,1},{18,2},{19,3},{20,4},{21,5},{22,6},{23,7},{24,8},{25... | collective-permute-start | bytes 73736 | tf_op jit(solution)/shard_map/ppermute | solution.py:20
  206.0 3.9 %collective-permute-start.18 = (f32[3,16,18,1]{2,1,3,0:T(8,128)S(1)}, f32[3,16,18,1]{2,1,3,0:T(8,128)S(1)}, u32[]{:S(2)}, u32[]{:S(2)}) collective-permute-start(f32[3,16,18,1]{2,1,3,0:T(8,128)S(1)} %copy.190), channel_id=1, source_target_pairs={{0,1},{1,2},{2,3},{3,4},{4,5},{5,6},{6,7},{7,8},{8,9},{9,10},{10,1... | collective-permute-start | bytes 10376 | tf_op jit(solution)/shard_map/ppermute | solution.py:19
  208.5 5.7 %collective-permute-start.19 = (f32[3,16,18,1]{2,1,3,0:T(8,128)S(1)}, f32[3,16,18,1]{2,1,3,0:T(8,128)S(1)}, u32[]{:S(2)}, u32[]{:S(2)}) collective-permute-start(f32[3,16,18,1]{2,1,3,0:T(8,128)S(1)} %copy.191), channel_id=1, source_target_pairs={{1,0},{2,1},{3,2},{4,3},{5,4},{6,5},{7,6},{8,7},{9,8},{10,9},{11,1... | collective-permute-start | bytes 10376 | tf_op jit(solution)/shard_map/ppermute | solution.py:20
  274.2 5.9 %collective-permute-start.20 = (f32[3,16,1,128]{3,1,2,0:T(8,128)S(1)}, f32[3,16,1,128]{3,1,2,0:T(8,128)S(1)}, u32[]{:S(2)}, u32[]{:S(2)}) collective-permute-start(f32[3,16,1,128]{3,1,2,0:T(8,128)S(1)} %get-tuple-element.100), channel_id=1, source_target_pairs={{0,16},{1,17},{2,18},{3,19},{4,20},{5,21},{6,22},{7,23},{8,24},{9,... | collective-permute-start | bytes 73736 | tf_op jit(solution)/shard_map/ppermute | solution.py:19
  278.6 5.7 %collective-permute-start.21 = (f32[3,16,1,128]{3,1,2,0:T(8,128)S(1)}, f32[3,16,1,128]{3,1,2,0:T(8,128)S(1)}, u32[]{:S(2)}, u32[]{:S(2)}) collective-permute-start(f32[3,16,1,128]{3,1,2,0:T(8,128)S(1)} %get-tuple-element.101), channel_id=1, source_target_pairs={{16,0},{17,1},{18,2},{19,3},{20,4},{21,5},{22,6},{23,7},{24,8},{25... | collective-permute-start | bytes 73736 | tf_op jit(solution)/shard_map/ppermute | solution.py:20
  285.0 3.9 %collective-permute-start.22 = (f32[3,16,18,1]{2,1,3,0:T(8,128)S(1)}, f32[3,16,18,1]{2,1,3,0:T(8,128)S(1)}, u32[]{:S(2)}, u32[]{:S(2)}) collective-permute-start(f32[3,16,18,1]{2,1,3,0:T(8,128)S(1)} %copy.192), channel_id=1, source_target_pairs={{0,1},{1,2},{2,3},{3,4},{4,5},{5,6},{6,7},{7,8},{8,9},{9,10},{10,1... | collective-permute-start | bytes 10376 | tf_op jit(solution)/shard_map/ppermute | solution.py:19
  287.3 5.7 %collective-permute-start.23 = (f32[3,16,18,1]{2,1,3,0:T(8,128)S(1)}, f32[3,16,18,1]{2,1,3,0:T(8,128)S(1)}, u32[]{:S(2)}, u32[]{:S(2)}) collective-permute-start(f32[3,16,18,1]{2,1,3,0:T(8,128)S(1)} %copy.193), channel_id=1, source_target_pairs={{1,0},{2,1},{3,2},{4,3},{5,4},{6,5},{7,6},{8,7},{9,8},{10,9},{11,1... | collective-permute-start | bytes 10376 | tf_op jit(solution)/shard_map/ppermute | solution.py:20
  353.9 14.0 %all-to-all-start = ((f32[6,16,16,128]{3,2,0,1:T(8,128)}), f32[6,16,16,128]{3,2,0,1:T(8,128)S(1)}, u32[]{:S(2)}, u32[]{:S(2)}) async-start(f32[6,16,16,128]{3,2,0,1:T(8,128)} %copy.186), calls=%async_computation | async-start | bytes 1572864 | tf_op jit(solution)/shard_map/all_to_all | solution.py:162
where the time goes:
time: 373 us; the launch traced here: 371 us
  blocking collectives  120 us (32%)
  other arithmetic  94.1 us (25%)
  waiting for transfers between devices  72.8 us (20%)
  starting transfers between devices  58.9 us (16%)
  local copies, waits for them, and re-layouts  13.6 us (4%)
  between operations  11.3 us (3%)
    psum x3, blocking collectives, two_products(): lax.psum((jnp.sum(residual * residual), jnp.sum(residual * image)), ('gx'...  120 us
    ppermute x12, waiting for transfers between devices, padded(): after = lax.ppermute(initial, axis, down)  47.1 us
    another operation x9, other arithmetic, apply_operator(): return jnp.stack(parts)  42.9 us
    ppermute x12, starting transfers between devices, padded(): before = lax.ppermute(last, axis, up)  39.2 us
    ppermute x12, starting transfers between devices, padded(): after = lax.ppermute(initial, axis, down)  16.1 us
    ppermute x12, waiting for transfers between devices, padded(): before = lax.ppermute(last, axis, up)  16 us
    mul x1, other arithmetic, per_device(): strain = lookup(substance_label, substance_traits[3], count) * warmed_result  15.6 us
    add x1, other arithmetic, heat_step(): return centre + time_step * inverse_cap * (heat_flux + power)  13 us
  transfers between devices with their start and end apart: 25, of which 21 were waited for; matrix products, arithmetic and copies ran while one was open for 1% of the time, Pallas kernels for 0%

commit v1 on v0

--- a/solution.py
+++ b/solution.py
@@ -7,6 +7,12 @@
 time_step = 0.03
 anchor_scale = 0.5
 strain_gain = 2.0
+
+
+def _solve_strings(t0):
+    for h in (("gy", "gz"), "gx"):
+        t0 = lax.psum(t0, h)
+    return t0
 
 
 def padded(value, sides, width):
@@ -108,7 +114,7 @@
 
 
 def two_products(residual, image):
-    return lax.psum((jnp.sum(residual * residual), jnp.sum(residual * image)), ("gx", "gy", "gz"))
+    return _solve_strings((jnp.sum(residual * residual), jnp.sum(residual * image)))
 
 
 def per_device(

time: 373 us -> 359 us (0.962)
  blocking collectives: 120 us -> 107 us
    psum x3 -> x6, blocking collectives: 120 us -> 107 us  [_solve_strings(): t0 = lax.psum(t0, h)]
where the time goes in v1:
time: 359 us; the launch traced here: 357 us
  blocking collectives  107 us (30%)
  other arithmetic  96 us (27%)
  waiting for transfers between devices  70.7 us (20%)
  starting transfers between devices  57.9 us (16%)
  local copies, waits for them, and re-layouts  13.6 us (4%)
  between operations  11.3 us (3%)
    psum x6, blocking collectives, _solve_strings(): t0 = lax.psum(t0, h)  107 us
    ppermute x12, waiting for transfers between devices, padded(): after = lax.ppermute(initial, axis, down)  47.1 us
    another operation x9, other arithmetic, apply_operator(): return jnp.stack(parts)  44.1 us
    ppermute x12, starting transfers between devices, padded(): before = lax.ppermute(last, axis, up)  38.2 us
    ppermute x12, starting transfers between devices, padded(): after = lax.ppermute(initial, axis, down)  16.1 us
    ppermute x12, waiting for transfers between devices, padded(): before = lax.ppermute(last, axis, up)  16 us
    mul x1, other arithmetic, per_device(): strain = lookup(substance_label, substance_traits[3], count) * warmed_result  15.6 us
    add x1, other arithmetic, heat_step(): return centre + time_step * inverse_cap * (heat_flux + power)  13 us
  transfers between devices with their start and end apart: 25, of which 21 were waited for; matrix products, arithmetic and copies ran while one was open for 1% of the time, Pallas kernels for 0%

profile of v1, /device:TPU:0, one launch (start us, length us, event | category | flops | bytes accessed | tf_op | source)
XLA Modules:
  0.0 357.0 jit_solution(14091216128686443268)
XLA Ops:
  0.6 2.0 fusion.181
  2.6 3.6 %fusion.168 = (f32[1,16,16,128]{3,1,2,0:T(8,128)S(1)}, pred[16,16,128]{2,0,1:T(8,128)(4,1)S(1)}, pred[16,16,128]{2,0,1:T(8,128)(4,1)S(1)}, pred[16,16,128]{2,0,1:T(8,128)(4,1)S(1)}, pred[16,16,128]{2,0,1:T(8,128)(4,1)S(1)}) fusion(f32[]{:T(128)} %bitcast.31, f32[]{:T(128)} %bitcast.30, f32[]{:T(128)} %bitcast.29, f32[]{:T(128)} %bitcast.28, ...), kind=kLoop, calls=%fused_computation.644 | loop fusion | flops 360448 | bytes 393232 | tf_op jit(solution)/shard_map/stack | solution.py:137
  6.2 3.5 copy_bitcast_fusion
  9.8 4.9 %collective-permute-start = (f32[2,16,1,128]{3,1,2,0:T(8,128)S(1)}, f32[2,16,1,128]{3,1,2,0:T(8,128)S(1)}, u32[]{:S(2)}, u32[]{:S(2)}) collective-permute-start(f32[2,16,1,128]{3,1,2,0:T(8,128)S(1)} %get-tuple-element.118), channel_id=1, source_target_pairs={{0,16},{1,17},{2,18},{3,19},{4,20},{5,21},{6,22},{7,23},{8,24},{9,... | collective-permute-start | bytes 49160 | tf_op jit(solution)/shard_map/ppermute | solution.py:25
  16.1 4.2 %collective-permute-done.1 = f32[2,16,1,128]{3,1,2,0:T(8,128)S(1)} collective-permute-done((f32[2,16,1,128]{3,1,2,0:T(8,128)S(1)}, f32[2,16,1,128]{3,1,2,0:T(8,128)S(1)}, u32[]{:S(2)}, u32[]{:S(2)}) %collective-permute-start.1) | collective-permute-done | bytes 16416 | tf_op jit(solution)/shard_map/ppermute | solution.py:26
  20.5 3.4 collective-permute-start.2
  26.0 8.3 %collective-permute-done.2 = f32[2,16,18,1]{3,1,2,0:T(8,128)S(1)} collective-permute-done((f32[2,16,18,1]{3,1,2,0:T(8,128)S(1)}, f32[2,16,18,1]{3,1,2,0:T(8,128)S(1)}, u32[]{:S(2)}, u32[]{:S(2)}) %collective-permute-start.2) | collective-permute-done | bytes 2336 | tf_op jit(solution)/shard_map/ppermute | solution.py:25
  35.5 13.0 %fusion.8 = f32[16,16,128]{2,0,1:T(8,128)S(1)} fusion(f32[16,16,128]{2,0,1:T(8,128)S(1)} %slice.2049, f32[16,18,130]{2,0,1:T(8,128)S(1)} %get-tuple-element.97, pred[16,16,128]{2,0,1:T(8,128)(4,1)S(1)} %get-tuple-element.80, f32[]{:T(128)} %bitcast.10, pred[16,16,128]{2,0,1:T(8,128)(4,1)S(1)} %get-tuple-element.79, f32[]{:T(128)} %bitcast.9, ...), kind=kLoop, calls=%fused_computation.73 | loop fusion | flops 3342336 | bytes 1835088 | tf_op jit(solution)/shard_map/add | solution.py:61
  51.5 4.2 %collective-permute-done.5 = f32[16,1,128]{2,0,1:T(8,128)S(1)} collective-permute-done((f32[16,1,128]{2,0,1:T(8,128)S(1)}, f32[16,1,128]{2,0,1:T(8,128)S(1)}, u32[]{:S(2)}, u32[]{:S(2)}) %collective-permute-start.5) | collective-permute-done | bytes 8224 | tf_op jit(solution)/shard_map/ppermute | solution.py:26
  55.8 4.8 %collective-permute-start.6 = (f32[16,18,1]{2,0,1:T(8,128)S(1)}, f32[16,18,1]{2,0,1:T(8,128)S(1)}, u32[]{:S(2)}, u32[]{:S(2)}) collective-permute-start(f32[16,18,1]{2,0,1:T(8,128)S(1)} %get-tuple-element.120), channel_id=1, source_target_pairs={{0,1},{1,2},{2,3},{3,4},{4,5},{5,6},{6,7},{7,8},{8,9},{9,10},{10,1... | collective-permute-start | bytes 3464 | tf_op jit(solution)/shard_map/ppermute | solution.py:25
  63.5 5.1 %collective-permute-done.7 = f32[16,18,1]{2,0,1:T(8,128)S(1)} collective-permute-done((f32[16,18,1]{2,0,1:T(8,128)S(1)}, f32[16,18,1]{2,0,1:T(8,128)S(1)}, u32[]{:S(2)}, u32[]{:S(2)}) %collective-permute-start.7) | collective-permute-done | bytes 1184 | tf_op jit(solution)/shard_map/ppermute | solution.py:26
  68.6 15.6 %add_multiply_fusion.6 = (f32[16,16,128]{2,0,1:T(8,128)S(1)}, f32[16,16,128]{2,0,1:T(8,128)S(1)}) fusion(pred[16,16,128]{2,0,1:T(8,128)(4,1)S(1)} %get-tuple-element.80, pred[16,16,128]{2,0,1:T(8,128)(4,1)S(1)} %get-tuple-element.79, pred[16,16,128]{2,0,1:T(8,128)(4,1)S(1)} %get-tuple-element.78, pred[16,16,128]{2,0,1:T(8,128)(4,1)S(1)} %get-tuple-element.77, ...), kind=kLoop, calls=%fused_computation.625 | loop fusion | flops 3866624 | bytes 1460576 | tf_op jit(solution)/shard_map/mul | solution.py:136
  84.1 1.6 collective-permute-start.8
  87.2 4.2 %collective-permute-done.9 = f32[2,16,1,128]{3,1,2,0:T(8,128)S(1)} collective-permute-done((f32[2,16,1,128]{3,1,2,0:T(8,128)S(1)}, f32[2,16,1,128]{3,1,2,0:T(8,128)S(1)}, u32[]{:S(2)}, u32[]{:S(2)}) %collective-permute-start.9) | collective-permute-done | bytes 16416 | tf_op jit(solution)/shard_map/ppermute | solution.py:26
  94.4 5.2 %collective-permute-done.10 = f32[2,16,18,1]{3,1,2,0:T(8,128)S(1)} collective-permute-done((f32[2,16,18,1]{3,1,2,0:T(8,128)S(1)}, f32[2,16,18,1]{3,1,2,0:T(8,128)S(1)}, u32[]{:S(2)}, u32[]{:S(2)}) %collective-permute-start.10) | collective-permute-done | bytes 2336 | tf_op jit(solution)/shard_map/ppermute | solution.py:25
  99.5 4.7 %collective-permute-done.11 = f32[2,16,18,1]{3,1,2,0:T(8,128)S(1)} collective-permute-done((f32[2,16,18,1]{3,1,2,0:T(8,128)S(1)}, f32[2,16,18,1]{3,1,2,0:T(8,128)S(1)}, u32[]{:S(2)}, u32[]{:S(2)}) %collective-permute-start.11) | collective-permute-done | bytes 2336 | tf_op jit(solution)/shard_map/ppermute | solution.py:26
  104.7 3.5 fusion.31
  108.2 3.6 fusion.52
  111.8 3.5 fusion.93
  115.3 2.2 collective-permute-start.12
  119.1 4.2 %collective-permute-done.13 = f32[3,16,1,128]{3,1,2,0:T(8,128)S(1)} collective-permute-done((f32[3,16,1,128]{3,1,2,0:T(8,128)S(1)}, f32[3,16,1,128]{3,1,2,0:T(8,128)S(1)}, u32[]{:S(2)}, u32[]{:S(2)}) %collective-permute-start.13) | collective-permute-done | bytes 24608 | tf_op jit(solution)/shard_map/ppermute | solution.py:26
  123.9 6.3 %collective-permute-start.14 = (f32[3,16,18,1]{2,1,3,0:T(8,128)S(1)}, f32[3,16,18,1]{2,1,3,0:T(8,128)S(1)}, u32[]{:S(2)}, u32[]{:S(2)}) collective-permute-start(f32[3,16,18,1]{2,1,3,0:T(8,128)S(1)} %copy.174), channel_id=1, source_target_pairs={{0,1},{1,2},{2,3},{3,4},{4,5},{5,6},{6,7},{7,8},{8,9},{9,10},{10,1... | collective-permute-start | bytes 10376 | tf_op jit(solution)/shard_map/ppermute | solution.py:25
  132.5 3.9 %collective-permute-done.15 = f32[3,16,18,1]{2,1,3,0:T(8,128)S(1)} collective-permute-done((f32[3,16,18,1]{2,1,3,0:T(8,128)S(1)}, f32[3,16,18,1]{2,1,3,0:T(8,128)S(1)}, u32[]{:S(2)}, u32[]{:S(2)}) %collective-permute-start.15) | collective-permute-done | bytes 3488 | tf_op jit(solution)/shard_map/ppermute | solution.py:26
  137.6 5.3 %add_bitcast_fusion.7 = f32[1,16,16,128]{3,1,2,0:T(8,128)S(1)} fusion(f32[16,16,128]{2,0,1:T(8,128)S(1)} %fusion.52, f32[16,16,128]{2,0,1:T(8,128)S(1)} %fusion.93, f32[18,18,130]{2,0,1:T(8,128)S(1)} %get-tuple-element.91, f32[18,18,130]{2,0,1:T(8,128)S(1)} %get-tuple-element.90, f32[16,16,128]{2,0,1:T(8,128)S(1)} %fusion.31, ...), kind=kLoop, calls=%fused_computation.599 | loop fusion | flops 11862016 | bytes 14286864 | tf_op jit(solution)/shard_map/stack | solution.py:95
  143.0 5.3 %add_bitcast_fusion.6 = f32[1,16,16,128]{3,1,2,0:T(8,128)S(1)} fusion(f32[16,16,128]{2,0,1:T(8,128)S(1)} %fusion.31, f32[16,16,128]{2,0,1:T(8,128)S(1)} %fusion.93, f32[18,18,130]{2,0,1:T(8,128)S(1)} %get-tuple-element.91, f32[16,16,128]{2,0,1:T(8,128)S(1)} %fusion.52, f32[18,18,130]{2,0,1:T(8,128)S(1)} %get-tuple-element.90, ...), kind=kLoop, calls=%fused_computation.598 | loop fusion | flops 11862016 | bytes 14286864 | tf_op jit(solution)/shard_map/stack | solution.py:95
  148.3 5.3 %add_bitcast_fusion.8 = f32[1,16,16,128]{3,1,2,0:T(8,128)S(1)} fusion(f32[16,16,128]{2,0,1:T(8,128)S(1)} %fusion.93, f32[18,18,130]{2,0,1:T(8,128)S(1)} %get-tuple-element.91, f32[16,16,128]{2,0,1:T(8,128)S(1)} %fusion.52, f32[18,18,130]{2,0,1:T(8,128)S(1)} %get-tuple-element.90, f32[16,16,128]{2,0,1:T(8,128)S(1)} %fusion.31, ...), kind=kLoop, calls=%fused_computation.600 | loop fusion | flops 11862016 | bytes 14286864 | tf_op jit(solution)/shard_map/stack | solution.py:95
  154.4 30.5 %all-reduce.9 = (f32[]{:T(128)}, f32[]{:T(128)}) all-reduce(f32[]{:T(128)} %get-tuple-element.17, f32[]{:T(128)} %get-tuple-element.16), channel_id=1, replica_groups=mesh['gx'=2,'gy'=8,'gz'=2] {'gy','gz'}, use_global_device_ids=true, to_apply=%region_1.2 | all-reduce | flops 2 | bytes 16 | tf_op jit(solution)/shard_map/psum | solution.py:14
  184.9 5.5 %all-reduce.12 = (f32[]{:T(128)}, f32[]{:T(128)}) all-reduce(f32[]{:T(128)} %get-tuple-element.22, f32[]{:T(128)} %get-tuple-element.23), channel_id=1, replica_groups=mesh['gx'=2,'gy'=8,'gz'=2] {'gx'}, use_global_device_ids=true, to_apply=%region_2.3 | all-reduce | flops 2 | bytes 16 | tf_op jit(solution)/shard_map/psum | solution.py:14
  191.8 1.9 collective-permute-start.16
  195.2 4.2 %collective-permute-done.17 = f32[3,16,1,128]{3,1,2,0:T(8,128)S(1)} collective-permute-done((f32[3,16,1,128]{3,1,2,0:T(8,128)S(1)}, f32[3,16,1,128]{3,1,2,0:T(8,128)S(1)}, u32[]{:S(2)}, u32[]{:S(2)}) %collective-permute-start.17) | collective-permute-done | bytes 24608 | tf_op jit(solution)/shard_map/ppermute | solution.py:26
  200.1 3.8 %collective-permute-start.18 = (f32[3,16,18,1]{2,1,3,0:T(8,128)S(1)}, f32[3,16,18,1]{2,1,3,0:T(8,128)S(1)}, u32[]{:S(2)}, u32[]{:S(2)}) collective-permute-start(f32[3,16,18,1]{2,1,3,0:T(8,128)S(1)} %copy.190), channel_id=1, source_target_pairs={{0,1},{1,2},{2,3},{3,4},{4,5},{5,6},{6,7},{7,8},{8,9},{9,10},{10,1... | collective-permute-start | bytes 10376 | tf_op jit(solution)/shard_map/ppermute | solution.py:25
  206.2 3.8 %collective-permute-done.19 = f32[3,16,18,1]{2,1,3,0:T(8,128)S(1)} collective-permute-done((f32[3,16,18,1]{2,1,3,0:T(8,128)S(1)}, f32[3,16,18,1]{2,1,3,0:T(8,128)S(1)}, u32[]{:S(2)}, u32[]{:S(2)}) %collective-permute-start.19) | collective-permute-done | bytes 3488 | tf_op jit(solution)/shard_map/ppermute | solution.py:26
  211.1 5.5 %add_bitcast_fusion.5 = (f32[1,16,16,128]{3,1,2,0:T(8,128)S(1)}, f32[16,16,128]{2,0,1:T(8,128)S(1)}, f32[16,16,128]{2,0,1:T(8,128)S(1)}, f32[16,16,128]{2,0,1:T(...) fusion(f32[18,18,130]{2,0,1:T(8,128)S(1)} %get-tuple-element.88, ...), kind=kLoop, calls=%fused_computation.573 | loop fusion | flops 11862016 | bytes 17170448 | tf_op jit(solution)/shard_map/stack | solution.py:95
  216.6 4.3 %add_bitcast_fusion.4 = f32[1,16,16,128]{3,1,2,0:T(8,128)S(1)} fusion(f32[16,16,128]{2,0,1:T(8,128)S(1)} %get-tuple-element.75, f32[16,16,128]{2,0,1:T(8,128)S(1)} %get-tuple-element.57, f32[16,16,128]{2,0,1:T(8,128)S(1)} %get-tuple-element.72, f32[16,16,128]{2,0,1:T(8,128)S(1)} %get-tuple-element.56, f32[16,16,128]{2,0,1:T(8,128)S(1)} %get-tuple-element.71, ...), kind=kLoop, calls=%fused_computation.572 | loop fusion | flops 7864320 | bytes 11403280 | tf_op jit(solution)/shard_map/stack | solution.py:95
  220.9 4.3 %add_bitcast_fusion.3 = f32[1,16,16,128]{3,1,2,0:T(8,128)S(1)} fusion(f32[16,16,128]{2,0,1:T(8,128)S(1)} %get-tuple-element.75, f32[16,16,128]{2,0,1:T(8,128)S(1)} %get-tuple-element.74, f32[16,16,128]{2,0,1:T(8,128)S(1)} %get-tuple-element.73, f32[16,16,128]{2,0,1:T(8,128)S(1)} %get-tuple-element.72, f32[16,16,128]{2,0,1:T(8,128)S(1)} %get-tuple-element.71, ...), kind=kLoop, calls=%fused_computation.571 | loop fusion | flops 7864320 | bytes 11403280 | tf_op jit(solution)/shard_map/stack | solution.py:95
  226.0 30.1 %all-reduce.8 = (f32[]{:T(128)}, f32[]{:T(128)}) all-reduce(f32[]{:T(128)} %get-tuple-element.15, f32[]{:T(128)} %get-tuple-element.14), channel_id=1, replica_groups=mesh['gx'=2,'gy'=8,'gz'=2] {'gy','gz'}, use_global_device_ids=true, to_apply=%region_7.8 | all-reduce | flops 2 | bytes 16 | tf_op jit(solution)/shard_map/psum | solution.py:14
  256.1 5.6 %all-reduce.11 = (f32[]{:T(128)}, f32[]{:T(128)}) all-reduce(f32[]{:T(128)} %get-tuple-element.20, f32[]{:T(128)} %get-tuple-element.21), channel_id=1, replica_groups=mesh['gx'=2,'gy'=8,'gz'=2] {'gx'}, use_global_device_ids=true, to_apply=%region_8.9 | all-reduce | flops 2 | bytes 16 | tf_op jit(solution)/shard_map/psum | solution.py:14
  266.6 1.9 collective-permute-start.20
  270.0 4.2 %collective-permute-done.21 = f32[3,16,1,128]{3,1,2,0:T(8,128)S(1)} collective-permute-done((f32[3,16,1,128]{3,1,2,0:T(8,128)S(1)}, f32[3,16,1,128]{3,1,2,0:T(8,128)S(1)}, u32[]{:S(2)}, u32[]{:S(2)}) %collective-permute-start.21) | collective-permute-done | bytes 24608 | tf_op jit(solution)/shard_map/ppermute | solution.py:26
  274.8 4.2 %collective-permute-start.22 = (f32[3,16,18,1]{2,1,3,0:T(8,128)S(1)}, f32[3,16,18,1]{2,1,3,0:T(8,128)S(1)}, u32[]{:S(2)}, u32[]{:S(2)}) collective-permute-start(f32[3,16,18,1]{2,1,3,0:T(8,128)S(1)} %copy.192), channel_id=1, source_target_pairs={{0,1},{1,2},{2,3},{3,4},{4,5},{5,6},{6,7},{7,8},{8,9},{9,10},{10,1... | collective-permute-start | bytes 10376 | tf_op jit(solution)/shard_map/ppermute | solution.py:25
  281.4 3.7 %collective-permute-done.23 = f32[3,16,18,1]{2,1,3,0:T(8,128)S(1)} collective-permute-done((f32[3,16,18,1]{2,1,3,0:T(8,128)S(1)}, f32[3,16,18,1]{2,1,3,0:T(8,128)S(1)}, u32[]{:S(2)}, u32[]{:S(2)}) %collective-permute-start.23) | collective-permute-done | bytes 3488 | tf_op jit(solution)/shard_map/ppermute | solution.py:26
  286.2 5.5 %add_bitcast_fusion.2 = (f32[1,16,16,128]{3,1,2,0:T(8,128)S(1)}, f32[16,16,128]{2,0,1:T(8,128)S(1)}, f32[16,16,128]{2,0,1:T(8,128)S(1)}, f32[16,16,128]{2,0,1:T(...) fusion(f32[18,18,130]{2,0,1:T(8,128)S(1)} %get-tuple-element.85, ...), kind=kLoop, calls=%fused_computation.546 | loop fusion | flops 11862016 | bytes 17170448 | tf_op jit(solution)/shard_map/stack | solution.py:95
  291.7 4.3 %add_bitcast_fusion.1 = f32[1,16,16,128]{3,1,2,0:T(8,128)S(1)} fusion(f32[16,16,128]{2,0,1:T(8,128)S(1)} %get-tuple-element.52, f32[16,16,128]{2,0,1:T(8,128)S(1)} %get-tuple-element.34, f32[16,16,128]{2,0,1:T(8,128)S(1)} %get-tuple-element.49, f32[16,16,128]{2,0,1:T(8,128)S(1)} %get-tuple-element.33, f32[16,16,128]{2,0,1:T(8,128)S(1)} %get-tuple-element.48, ...), kind=kLoop, calls=%fused_computation.545 | loop fusion | flops 7864320 | bytes 11403280 | tf_op jit(solution)/shard_map/stack | solution.py:95
  296.0 4.3 %add_bitcast_fusion = f32[1,16,16,128]{3,1,2,0:T(8,128)S(1)} fusion(f32[16,16,128]{2,0,1:T(8,128)S(1)} %get-tuple-element.52, f32[16,16,128]{2,0,1:T(8,128)S(1)} %get-tuple-element.51, f32[16,16,128]{2,0,1:T(8,128)S(1)} %get-tuple-element.50, f32[16,16,128]{2,0,1:T(8,128)S(1)} %get-tuple-element.49, f32[16,16,128]{2,0,1:T(8,128)S(1)} %get-tuple-element.48, ...), kind=kLoop, calls=%fused_computation.544 | loop fusion | flops 7864320 | bytes 11403280 | tf_op jit(solution)/shard_map/stack | solution.py:95
  301.1 30.1 %all-reduce.7 = (f32[]{:T(128)}, f32[]{:T(128)}) all-reduce(f32[]{:T(128)} %get-tuple-element.13, f32[]{:T(128)} %get-tuple-element.12), channel_id=1, replica_groups=mesh['gx'=2,'gy'=8,'gz'=2] {'gy','gz'}, use_global_device_ids=true, to_apply=%region_13.14 | all-reduce | flops 2 | bytes 16 | tf_op jit(solution)/shard_map/psum | solution.py:14
  331.2 5.5 %all-reduce.10 = (f32[]{:T(128)}, f32[]{:T(128)}) all-reduce(f32[]{:T(128)} %get-tuple-element.18, f32[]{:T(128)} %get-tuple-element.19), channel_id=1, replica_groups=mesh['gx'=2,'gy'=8,'gz'=2] {'gx'}, use_global_device_ids=true, to_apply=%region_14.15 | all-reduce | flops 2 | bytes 16 | tf_op jit(solution)/shard_map/psum | solution.py:14
  342.3 3.5 all-to-all-start
  346.6 7.6 %all-to-all-done = f32[6,16,16,128]{3,2,0,1:T(8,128)S(1)} async-done(((f32[6,16,16,128]{3,2,0,1:T(8,128)}), f32[6,16,16,128]{3,2,0,1:T(8,128)S(1)}, u32[]{:S(2)}, u32[]{:S(2)}) %all-to-all-start) | async-done | bytes 786464 | tf_op jit(solution)/shard_map/all_to_all | solution.py:168
  (87 shorter events, 39.6 us)
Async XLA Ops:
  6.2 19.0 %copy-start.1 = (f32[16]{0:T(128)S(1)}, f32[16]{0:T(128)}, u32[]{:S(2)}) copy-start(f32[16]{0:T(128)} %param.9) | copy-start | bytes 196
  9.8 6.3 %collective-permute-start = (f32[2,16,1,128]{3,1,2,0:T(8,128)S(1)}, f32[2,16,1,128]{3,1,2,0:T(8,128)S(1)}, u32[]{:S(2)}, u32[]{:S(2)}) collective-permute-start(f32[2,16,1,128]{3,1,2,0:T(8,128)S(1)} %get-tuple-element.118), channel_id=1, source_target_pairs={{0,16},{1,17},{2,18},{3,19},{4,20},{5,21},{6,22},{7,23},{8,24},{9,... | collective-permute-start | bytes 49160 | tf_op jit(solution)/shard_map/ppermute | solution.py:25
  14.7 5.6 %collective-permute-start.1 = (f32[2,16,1,128]{3,1,2,0:T(8,128)S(1)}, f32[2,16,1,128]{3,1,2,0:T(8,128)S(1)}, u32[]{:S(2)}, u32[]{:S(2)}) collective-permute-start(f32[2,16,1,128]{3,1,2,0:T(8,128)S(1)} %get-tuple-element.119), channel_id=1, source_target_pairs={{16,0},{17,1},{18,2},{19,3},{20,4},{21,5},{22,6},{23,7},{24,8},{25... | collective-permute-start | bytes 49160 | tf_op jit(solution)/shard_map/ppermute | solution.py:26
  20.5 13.8 %collective-permute-start.2 = (f32[2,16,18,1]{3,1,2,0:T(8,128)S(1)}, f32[2,16,18,1]{3,1,2,0:T(8,128)S(1)}, u32[]{:S(2)}, u32[]{:S(2)}) collective-permute-start(f32[2,16,18,1]{3,1,2,0:T(8,128)S(1)} %get-tuple-element.114), channel_id=1, source_target_pairs={{0,1},{1,2},{2,3},{3,4},{4,5},{5,6},{6,7},{7,8},{8,9},{9,10},{10,1... | collective-permute-start | bytes 6920 | tf_op jit(solution)/shard_map/ppermute | solution.py:25
  23.9 11.0 %collective-permute-start.3 = (f32[2,16,18,1]{3,1,2,0:T(8,128)S(1)}, f32[2,16,18,1]{3,1,2,0:T(8,128)S(1)}, u32[]{:S(2)}, u32[]{:S(2)}) collective-permute-start(f32[2,16,18,1]{3,1,2,0:T(8,128)S(1)} %get-tuple-element.115), channel_id=1, source_target_pairs={{1,0},{2,1},{3,2},{4,3},{5,4},{6,5},{7,6},{8,7},{9,8},{10,9},{11,1... | collective-permute-start | bytes 6920 | tf_op jit(solution)/shard_map/ppermute | solution.py:26
  25.9 9.5 %copy-start = (s32[16,16,128]{2,1,0:T(8,128)S(1)}, s32[16,16,128]{2,1,0:T(8,128)}, u32[]{:S(2)}) copy-start(s32[16,16,128]{2,1,0:T(8,128)} %param.7) | copy-start | bytes 393220
  48.5 3.0 collective-permute-start.4
  50.2 5.5 %collective-permute-start.5 = (f32[16,1,128]{2,0,1:T(8,128)S(1)}, f32[16,1,128]{2,0,1:T(8,128)S(1)}, u32[]{:S(2)}, u32[]{:S(2)}) collective-permute-start(f32[16,1,128]{2,0,1:T(8,128)S(1)} %get-tuple-element.123), channel_id=1, source_target_pairs={{16,0},{17,1},{18,2},{19,3},{20,4},{21,5},{22,6},{23,7},{24,8},{25... | collective-permute-start | bytes 24584 | tf_op jit(solution)/shard_map/ppermute | solution.py:26
  55.8 7.7 %collective-permute-start.6 = (f32[16,18,1]{2,0,1:T(8,128)S(1)}, f32[16,18,1]{2,0,1:T(8,128)S(1)}, u32[]{:S(2)}, u32[]{:S(2)}) collective-permute-start(f32[16,18,1]{2,0,1:T(8,128)S(1)} %get-tuple-element.120), channel_id=1, source_target_pairs={{0,1},{1,2},{2,3},{3,4},{4,5},{5,6},{6,7},{7,8},{8,9},{9,10},{10,1... | collective-permute-start | bytes 3464 | tf_op jit(solution)/shard_map/ppermute | solution.py:25
  60.7 7.9 %collective-permute-start.7 = (f32[16,18,1]{2,0,1:T(8,128)S(1)}, f32[16,18,1]{2,0,1:T(8,128)S(1)}, u32[]{:S(2)}, u32[]{:S(2)}) collective-permute-start(f32[16,18,1]{2,0,1:T(8,128)S(1)} %get-tuple-element.121), channel_id=1, source_target_pairs={{1,0},{2,1},{3,2},{4,3},{5,4},{6,5},{7,6},{8,7},{9,8},{10,9},{11,1... | collective-permute-start | bytes 3464 | tf_op jit(solution)/shard_map/ppermute | solution.py:26
  84.1 3.1 collective-permute-start.8
  85.8 5.6 %collective-permute-start.9 = (f32[2,16,1,128]{3,1,2,0:T(8,128)S(1)}, f32[2,16,1,128]{3,1,2,0:T(8,128)S(1)}, u32[]{:S(2)}, u32[]{:S(2)}) collective-permute-start(f32[2,16,1,128]{3,1,2,0:T(8,128)S(1)} %get-tuple-element.117), channel_id=1, source_target_pairs={{16,0},{17,1},{18,2},{19,3},{20,4},{21,5},{22,6},{23,7},{24,8},{25... | collective-permute-start | bytes 49160 | tf_op jit(solution)/shard_map/ppermute | solution.py:26
  91.6 7.9 %collective-permute-start.10 = (f32[2,16,18,1]{3,1,2,0:T(8,128)S(1)}, f32[2,16,18,1]{3,1,2,0:T(8,128)S(1)}, u32[]{:S(2)}, u32[]{:S(2)}) collective-permute-start(f32[2,16,18,1]{3,1,2,0:T(8,128)S(1)} %get-tuple-element.112), channel_id=1, source_target_pairs={{0,1},{1,2},{2,3},{3,4},{4,5},{5,6},{6,7},{7,8},{8,9},{9,10},{10,1... | collective-permute-start | bytes 6920 | tf_op jit(solution)/shard_map/ppermute | solution.py:25
  93.1 11.1 %collective-permute-start.11 = (f32[2,16,18,1]{3,1,2,0:T(8,128)S(1)}, f32[2,16,18,1]{3,1,2,0:T(8,128)S(1)}, u32[]{:S(2)}, u32[]{:S(2)}) collective-permute-start(f32[2,16,18,1]{3,1,2,0:T(8,128)S(1)} %get-tuple-element.113), channel_id=1, source_target_pairs={{1,0},{2,1},{3,2},{4,3},{5,4},{6,5},{7,6},{8,7},{9,8},{10,9},{11,1... | collective-permute-start | bytes 6920 | tf_op jit(solution)/shard_map/ppermute | solution.py:26
  115.3 3.7 %collective-permute-start.12 = (f32[3,16,1,128]{3,1,2,0:T(8,128)S(1)}, f32[3,16,1,128]{3,1,2,0:T(8,128)S(1)}, u32[]{:S(2)}, u32[]{:S(2)}) collective-permute-start(f32[3,16,1,128]{3,1,2,0:T(8,128)S(1)} %get-tuple-element.110), channel_id=1, source_target_pairs={{0,16},{1,17},{2,18},{3,19},{4,20},{5,21},{6,22},{7,23},{8,24},{9,... | collective-permute-start | bytes 73736 | tf_op jit(solution)/shard_map/ppermute | solution.py:25
  117.6 5.7 %collective-permute-start.13 = (f32[3,16,1,128]{3,1,2,0:T(8,128)S(1)}, f32[3,16,1,128]{3,1,2,0:T(8,128)S(1)}, u32[]{:S(2)}, u32[]{:S(2)}) collective-permute-start(f32[3,16,1,128]{3,1,2,0:T(8,128)S(1)} %get-tuple-element.111), channel_id=1, source_target_pairs={{16,0},{17,1},{18,2},{19,3},{20,4},{21,5},{22,6},{23,7},{24,8},{25... | collective-permute-start | bytes 73736 | tf_op jit(solution)/shard_map/ppermute | solution.py:26
  123.9 8.2 %collective-permute-start.14 = (f32[3,16,18,1]{2,1,3,0:T(8,128)S(1)}, f32[3,16,18,1]{2,1,3,0:T(8,128)S(1)}, u32[]{:S(2)}, u32[]{:S(2)}) collective-permute-start(f32[3,16,18,1]{2,1,3,0:T(8,128)S(1)} %copy.174), channel_id=1, source_target_pairs={{0,1},{1,2},{2,3},{3,4},{4,5},{5,6},{6,7},{7,8},{8,9},{9,10},{10,1... | collective-permute-start | bytes 10376 | tf_op jit(solution)/shard_map/ppermute | solution.py:25
  130.7 5.8 %collective-permute-start.15 = (f32[3,16,18,1]{2,1,3,0:T(8,128)S(1)}, f32[3,16,18,1]{2,1,3,0:T(8,128)S(1)}, u32[]{:S(2)}, u32[]{:S(2)}) collective-permute-start(f32[3,16,18,1]{2,1,3,0:T(8,128)S(1)} %copy.175), channel_id=1, source_target_pairs={{1,0},{2,1},{3,2},{4,3},{5,4},{6,5},{7,6},{8,7},{9,8},{10,9},{11,1... | collective-permute-start | bytes 10376 | tf_op jit(solution)/shard_map/ppermute | solution.py:26
  191.8 3.4 collective-permute-start.16
  193.7 5.7 %collective-permute-start.17 = (f32[3,16,1,128]{3,1,2,0:T(8,128)S(1)}, f32[3,16,1,128]{3,1,2,0:T(8,128)S(1)}, u32[]{:S(2)}, u32[]{:S(2)}) collective-permute-start(f32[3,16,1,128]{3,1,2,0:T(8,128)S(1)} %get-tuple-element.109), channel_id=1, source_target_pairs={{16,0},{17,1},{18,2},{19,3},{20,4},{21,5},{22,6},{23,7},{24,8},{25... | collective-permute-start | bytes 73736 | tf_op jit(solution)/shard_map/ppermute | solution.py:26
  200.1 5.7 %collective-permute-start.18 = (f32[3,16,18,1]{2,1,3,0:T(8,128)S(1)}, f32[3,16,18,1]{2,1,3,0:T(8,128)S(1)}, u32[]{:S(2)}, u32[]{:S(2)}) collective-permute-start(f32[3,16,18,1]{2,1,3,0:T(8,128)S(1)} %copy.190), channel_id=1, source_target_pairs={{0,1},{1,2},{2,3},{3,4},{4,5},{5,6},{6,7},{7,8},{8,9},{9,10},{10,1... | collective-permute-start | bytes 10376 | tf_op jit(solution)/shard_map/ppermute | solution.py:25
  204.3 5.7 %collective-permute-start.19 = (f32[3,16,18,1]{2,1,3,0:T(8,128)S(1)}, f32[3,16,18,1]{2,1,3,0:T(8,128)S(1)}, u32[]{:S(2)}, u32[]{:S(2)}) collective-permute-start(f32[3,16,18,1]{2,1,3,0:T(8,128)S(1)} %copy.191), channel_id=1, source_target_pairs={{1,0},{2,1},{3,2},{4,3},{5,4},{6,5},{7,6},{8,7},{9,8},{10,9},{11,1... | collective-permute-start | bytes 10376 | tf_op jit(solution)/shard_map/ppermute | solution.py:26
  266.6 3.4 collective-permute-start.20
  268.5 5.7 %collective-permute-start.21 = (f32[3,16,1,128]{3,1,2,0:T(8,128)S(1)}, f32[3,16,1,128]{3,1,2,0:T(8,128)S(1)}, u32[]{:S(2)}, u32[]{:S(2)}) collective-permute-start(f32[3,16,1,128]{3,1,2,0:T(8,128)S(1)} %get-tuple-element.107), channel_id=1, source_target_pairs={{16,0},{17,1},{18,2},{19,3},{20,4},{21,5},{22,6},{23,7},{24,8},{25... | collective-permute-start | bytes 73736 | tf_op jit(solution)/shard_map/ppermute | solution.py:26
  274.8 6.1 %collective-permute-start.22 = (f32[3,16,18,1]{2,1,3,0:T(8,128)S(1)}, f32[3,16,18,1]{2,1,3,0:T(8,128)S(1)}, u32[]{:S(2)}, u32[]{:S(2)}) collective-permute-start(f32[3,16,18,1]{2,1,3,0:T(8,128)S(1)} %copy.192), channel_id=1, source_target_pairs={{0,1},{1,2},{2,3},{3,4},{4,5},{5,6},{6,7},{7,8},{8,9},{9,10},{10,1... | collective-permute-start | bytes 10376 | tf_op jit(solution)/shard_map/ppermute | solution.py:25
  279.4 5.7 %collective-permute-start.23 = (f32[3,16,18,1]{2,1,3,0:T(8,128)S(1)}, f32[3,16,18,1]{2,1,3,0:T(8,128)S(1)}, u32[]{:S(2)}, u32[]{:S(2)}) collective-permute-start(f32[3,16,18,1]{2,1,3,0:T(8,128)S(1)} %copy.193), channel_id=1, source_target_pairs={{1,0},{2,1},{3,2},{4,3},{5,4},{6,5},{7,6},{8,7},{9,8},{10,9},{11,1... | collective-permute-start | bytes 10376 | tf_op jit(solution)/shard_map/ppermute | solution.py:26
  342.3 11.9 %all-to-all-start = ((f32[6,16,16,128]{3,2,0,1:T(8,128)}), f32[6,16,16,128]{3,2,0,1:T(8,128)S(1)}, u32[]{:S(2)}, u32[]{:S(2)}) async-start(f32[6,16,16,128]{3,2,0,1:T(8,128)} %copy.186), calls=%async_computation | async-start | bytes 1572864 | tf_op jit(solution)/shard_map/all_to_all | solution.py:168
